TPU v7x, 32 devices: a whole 2x2x4 slice. The times are simulated.
32 devices in a mesh: groups: 2 (over x), cent: 16 (over z, y, core).
Axes of the slice: x: 2, y: 2, z: 4, core: 2. Of those that a mesh axis runs over, the one named last changes fastest.
Arguments:
- points: bfloat16 [1024, 768], P(('groups', 'cent')), parts along dimension 0, may hold values from -64 to 64, as said below
- centroids: bfloat16 [131072, 768], P(('groups', 'cent')), parts along dimension 0, may hold values from -1 to 1
- coarse_init: float32 [4096, 768], P(('groups', 'cent')), parts along dimension 0, may hold values from -2.4 to 2.4
- assign: int32 [131072], P(('groups', 'cent')), parts along dimension 0, may hold values from 0 to 2047, as said below
Outputs:
- level_one: bfloat16 [131072, 768], P(('groups', 'cent')), parts along dimension 0
- level_two: float32 [4096, 768], P(('groups', 'cent')), parts along dimension 0
There are 2 independent parts, one for each index of `groups`. A program takes and returns all parts, laid end to end along the dimension named above; each array names one. Nothing has to cross between parts.
Inputs may be any that keep to these rules, and one draw needn't show every extreme that they name: `points`: entries normal (clipped at 8) or uniform within 1.7; on some draws a few rows are scaled multiples of a centroid that has a close twin, giving logits up to about 300. `assign`: among the 65536 // 16 level-1 centroids held by one index of cent, at most 512 have their level-2 centroid in any one block of 2048 // 16 consecutive level-2 centroids, and some block receives exactly 512.
All inputs are finite; a program needn't handle non-finite values.
Results may differ from a plain program's by a relative error of at most 0.0039.
Values may be sent and summed in bfloat16 or wider, within the bound.
A program may use at most 64 MiB of HBM per device.

v0:
```python
import math
import jax
import jax.numpy as jnp
from jax import lax
from jax.sharding import PartitionSpec as P

D = 768
K2 = 2048
TEMP = 0.05
PRIOR_ONE = 0.02
PRIOR_TWO = 0.25


def shards(points, centroids, coarse_init, assign):
    scale = 1.0 / (TEMP * math.sqrt(D))
    everyone = lax.all_gather(points, "cent", axis=0, tiled=True)
    count = everyone.shape[0]
    rows = min(512, count)
    pblocks = everyone.reshape(count // rows, rows, D)
    local_k = centroids.shape[0]

    def logits_of(block):
        return (
            lax.dot_general(
                block, centroids, (((1,), (1,)), ((), ())), preferred_element_type=jnp.float32
            )
            * scale
        )

    def local_stats(block):
        logits = logits_of(block)
        top = jnp.max(logits, axis=1)
        return (top, jnp.sum(jnp.exp(logits - top[:, None]), axis=1))

    local_top, local_sum = lax.map(local_stats, pblocks)
    local_top = local_top.reshape(count)
    local_sum = local_sum.reshape(count)
    peak = lax.pmax(local_top, "cent")
    total = lax.psum(local_sum * jnp.exp(local_top - peak), "cent")
    peaks = peak.reshape(count // rows, rows)
    totals = total.reshape(count // rows, rows)

    def accumulate(carry, item):
        block, peak_rows, total_rows = item
        resp = jnp.exp(logits_of(block) - peak_rows[:, None]) / total_rows[:, None]
        mass = carry[0] + jnp.sum(resp, axis=0)
        weighted = carry[1] + lax.dot_general(
            resp.astype(jnp.bfloat16),
            block,
            (((0,), (0,)), ((), ())),
            preferred_element_type=jnp.float32,
        )
        return ((mass, weighted), None)

    start_carry = (jnp.zeros((local_k,), jnp.float32), jnp.zeros((local_k, D), jnp.float32))
    (mass, weighted), _ = lax.scan(accumulate, start_carry, (pblocks, peaks, totals))
    fresh = (weighted + PRIOR_ONE * centroids.astype(jnp.float32)) / (mass[:, None] + PRIOR_ONE)
    level_one = fresh.astype(jnp.bfloat16)
    moved = (mass[:, None] * fresh).astype(jnp.bfloat16)
    mass_high = mass.astype(jnp.bfloat16)
    mass_low = (mass - mass_high.astype(jnp.float32)).astype(jnp.bfloat16)
    onehot = (assign[:, None] == lax.broadcasted_iota(jnp.int32, (1, K2), 1)).astype(jnp.bfloat16)
    wsum_term = lax.dot_general(
        onehot, moved, (((0,), (0,)), ((), ())), preferred_element_type=jnp.float32
    )
    mass_pair = jnp.stack([mass_high, mass_low])
    msum_term = jnp.sum(jnp.dot(mass_pair, onehot, preferred_element_type=jnp.float32), axis=0)
    wsum, msum = (
        lax.psum_scatter(wsum_term, "cent", scatter_dimension=0, tiled=True),
        lax.psum_scatter(msum_term, "cent", scatter_dimension=0, tiled=True),
    )
    level_two = (wsum + PRIOR_TWO * coarse_init) / (msum[:, None] + PRIOR_TWO)
    return (level_one, level_two)


def solution(mesh):
    return jax.shard_map(
        shards,
        mesh=mesh,
        in_specs=(
            P(("groups", "cent"), None),
            P(("groups", "cent"), None),
            P(("groups", "cent"), None),
            P(("groups", "cent")),
        ),
        out_specs=(P(("groups", "cent"), None), P(("groups", "cent"), None)),
        check_vma=False,
    )
```

profile of v0, /device:TPU:0, one launch (start us, length us, event | category | flops | bytes accessed | tf_op | source)
XLA Modules:
  0.0 236.3 jit_solution(16250268285683801577)
XLA Ops:
  7.2 0.0 reduce-scatter.2.cloned.1.call-start
  7.2 25.7 %all_gather.3 = bf16[512,768]{1,0:T(8,128)(2,1)S(1)} all-gather(bf16[32,768]{1,0:T(8,128)(2,1)} %param.4), channel_id=1, replica_groups=mesh['groups'=2,'cent'=16] {'cent'}, dimensions={0}, use_global_device_ids=true | all-gather | bytes 835584 | tf_op jit(solution)/shard_map/all_gather | solution.py:16
  32.9 8.4 %multiply_reduce_fusion = (f32[512]{0:T(512)S(1)}, f32[512,4096]{1,0:T(8,128)}) fusion(bf16[512,768]{1,0:T(8,128)(2,1)S(1)} %all_gather.3, bf16[4096,768]{1,0:T(8,128)(2,1)} %param.5), kind=kOutput, calls=%fused_computation.9 | convolution fusion | flops 3225419264 | bytes 15468544 | tf_op jit(solution)/shard_map/while/body/eval_jaxpr/dot_general | solution.py:24
  41.4 29.8 %pmax.7 = f32[512]{0:T(512)S(1)} all-reduce(f32[512]{0:T(512)S(1)} %get-tuple-element.24), channel_id=1, replica_groups=mesh['groups'=2,'cent'=16] {'cent'}, use_global_device_ids=true, to_apply=%region_1.0 | all-reduce | flops 512 | bytes 4096 | tf_op jit(solution)/shard_map/pmax | solution.py:38
  71.2 4.9 %exponential_reduce_fusion = f32[512]{0:T(512)S(1)} fusion(f32[512,4096]{1,0:T(8,128)} %get-tuple-element.25, f32[512]{0:T(512)S(1)} %get-tuple-element.24), kind=kLoop, calls=%fused_computation.7 | loop fusion | flops 6290944 | bytes 8392704 | tf_op jit(solution)/shard_map/while/body/eval_jaxpr/reduce_sum | solution.py:33
  76.1 29.5 %psum.7 = f32[512]{0:T(512)S(1)} all-reduce(f32[512]{0:T(512)S(1)} %exponential_multiply_fusion), channel_id=1, replica_groups=mesh['groups'=2,'cent'=16] {'cent'}, use_global_device_ids=true, to_apply=%region_3.4 | all-reduce | flops 512 | bytes 4096 | tf_op jit(solution)/shard_map/psum | solution.py:39
  105.6 4.5 %fusion.11 = f32[4096]{0:T(1024)S(1)} fusion(f32[512]{0:T(512)S(1)} %psum.7, f32[512]{0:T(512)S(1)} %pmax.7, f32[512,4096]{1,0:T(8,128)} %get-tuple-element.25), kind=kLoop, calls=%fused_computation.22 | loop fusion | flops 8384512 | bytes 8409088 | tf_op jit(solution)/shard_map/while/body/eval_jaxpr/reduce_sum | solution.py:46
  110.1 0.0 copy-start.1
  110.1 12.1 %fusion.12 = (bf16[4096,768]{1,0:T(8,128)(2,1)}, f32[4096,768]{1,0:T(8,128)}) fusion(f32[4096]{0:T(1024)S(1)} %broadcast_add_fusion, bf16[4096,768]{1,0:T(8,128)(2,1)} %param.5, bf16[512,768]{1,0:T(8,128)(2,1)S(1)} %all_gather.3, f32[512]{0:T(512)S(1)} %psum.7, f32[512]{0:T(512)S(1)} %pmax.7, f32[512,4096]{1,0:T(8,128)} %get-tuple-element.25), kind=kOutput, calls=%fused_computation.23 | convolution fusion | flops 3245342720 | bytes 34361344 | tf_op jit(solution)/shard_map/while/body/eval_jaxpr/dot_general | solution.py:47
  122.1 0.0 copy-done.1
  122.1 0.0 copy-start.2
  122.1 22.7 %fusion.1 = f32[2048,768]{1,0:T(8,128)} fusion(s32[4096]{0:T(1024)S(1)} %copy-done.1, f32[4096,768]{1,0:T(8,128)} %get-tuple-element.34, f32[4096]{0:T(1024)S(1)} %fusion.11), kind=kOutput, calls=%fused_computation.2 | convolution fusion | flops 12899581952 | bytes 18907136 | tf_op jit(solution)/shard_map/dot_general | solution.py:63
  144.9 0.0 copy-start
  144.9 0.0 reduce-scatter.2.cloned.1.call-update
  144.9 0.0 copy-done.2
  145.0 0.6 dynamic-slice.3
  146.2 5.9 %fusion.6 = f32[2048]{0:T(1024)S(1)} fusion(s32[4096]{0:T(1024)S(1)} %copy-done.1, bf16[1,4096]{1,0:T(2,128)(2,1)S(1)} %subtract_convert_fusion, bf16[1,4096]{1,0:T(2,128)(2,1)S(1)} %convert_element_type.52), kind=kOutput, calls=%fused_computation.12 | convolution fusion | flops 41977856 | bytes 40960 | tf_op jit(solution)/shard_map/dot_general | solution.py:67
  152.1 30.7 %all-reduce = f32[2048]{0:T(1024)S(1)} all-reduce(f32[2048]{0:T(1024)S(1)} %fusion.6), channel_id=3, replica_groups=mesh['groups'=2,'cent'=16] {'cent'}, use_global_device_ids=true, to_apply=%region_7.8.clone | all-reduce | flops 2048 | bytes 16384
  182.8 0.1 dynamic-slice_add_fusion
  182.9 44.7 %reduce-scatter.2.cloned.1.call-done = f32[128,768]{1,0:T(8,128)} async-done(((f32[2048,768]{1,0:T(8,128)}), f32[128,768]{1,0:T(8,128)}) %reduce-scatter.2.cloned.1.call-update) | async-done | bytes 393232 | tf_op jit(solution)/shard_map/reduce_scatter | solution.py:69
  227.6 0.0 copy-done
  227.6 1.8 add_divide_fusion.1
  (4 shorter events, 0.0 us)
Async XLA Ops:
  7.2 220.5 %reduce-scatter.2.cloned.1.call-start = ((), (), s32[]{:S(2)}) async-start(), calls=%async_computation.1 | async-start | bytes 6684672 | tf_op jit(solution)/shard_map/reduce_scatter | solution.py:69
  110.1 12.1 %copy-start.1 = (s32[4096]{0:T(1024)S(1)}, s32[4096]{0:T(1024)}, u32[]{:S(2)}) copy-start(s32[4096]{0:T(1024)} %param.7) | copy-start | bytes 49156
  122.1 22.8 %copy-start.2 = (u32[32]{0:T(128)S(1)}, u32[32]{0:T(128)}, u32[]{:S(2)}) copy-start(u32[32]{0:T(128)} %constant.43) | copy-start | bytes 388
  144.9 82.8 %copy-start = (f32[128,768]{1,0:T(8,128)S(1)}, f32[128,768]{1,0:T(8,128)}, u32[]{:S(2)}) copy-start(f32[128,768]{1,0:T(8,128)} %param.6) | copy-start | bytes 1179652
Sparse Core Ops, SparseCore 0:
  145.0 82.5 reduce-scatter.1
where the time goes:
time: 237 us; the launch traced here: 236 us
  blocking collectives  116 us (49%)
  matrix products  49.1 us (21%)
  waiting for transfers between devices  44.8 us (19%)
  between operations  14.8 us (6%)
  other arithmetic  11.3 us (5%)
    reduce_scatter x1, waiting for transfers between devices, shards(): lax.psum_scatter(wsum_term, 'cent', scatter_dimension=0, tiled=True)  44.7 us
    unnamed x1, blocking collectives  30.7 us
    pmax x1, blocking collectives, shards(): peak = lax.pmax(local_top, 'cent')  29.8 us
    psum x1, blocking collectives, shards(): total = lax.psum(local_sum * jnp.exp(local_top - peak), 'cent')  29.5 us
    all_gather x1, blocking collectives, shards(): everyone = lax.all_gather(points, 'cent', axis=0, tiled=True)  25.7 us
    dot_general x1, matrix products, shards(): lax.dot_general(onehot, moved, (((0,), (0,)), ((), ())), preferred_elemen...  22.7 us
    dot_general x1, matrix products, accumulate(): lax.dot_general(resp.astype(jnp.bfloat16), block, (((0,), (0,)), ((), ())...  12.1 us
    dot_general x1, matrix products, logits_of(): lax.dot_general(block, centroids, (((1,), (1,)), ((), ())), preferred_ele...  8.45 us
  transfers between devices with their start and end apart: 1, of which 1 were waited for; matrix products, arithmetic and copies ran while one was open for 3% of the time, Pallas kernels for 0%

commit v1 on v0

--- a/solution.py
+++ b/solution.py
@@ -36,7 +36,9 @@
     local_top = local_top.reshape(count)
     local_sum = local_sum.reshape(count)
     peak = lax.pmax(local_top, "cent")
-    total = lax.psum(local_sum * jnp.exp(local_top - peak), "cent")
+    block_2 = local_sum * jnp.exp(local_top - peak)
+    terms = lax.all_gather(block_2, "cent")
+    total = jnp.sum(terms, axis=0)
     peaks = peak.reshape(count // rows, rows)
     totals = total.reshape(count // rows, rows)
 

time: 237 us -> 226 us (0.954)
  blocking collectives: 116 us -> 106 us
    psum x1 -> x0, blocking collectives: 29.5 us -> none  [shards(): total = lax.psum(local_sum * jnp.exp(local_top - peak), 'cent')]
    all_gather x0 -> x1, blocking collectives: none -> 17.2 us  [shards(): terms = lax.all_gather(block_2, 'cent')]
where the time goes in v1:
time: 226 us; the launch traced here: 225 us
  blocking collectives  106 us (47%)
  matrix products  49.1 us (22%)
  waiting for transfers between devices  44 us (19%)
  between operations  14.8 us (7%)
  other arithmetic  11.3 us (5%)
    reduce_scatter x1, waiting for transfers between devices, shards(): lax.psum_scatter(wsum_term, 'cent', scatter_dimension=0, tiled=True)  43.9 us
    unnamed x1, blocking collectives  32.9 us
    pmax x1, blocking collectives, shards(): peak = lax.pmax(local_top, 'cent')  29.8 us
    all_gather x1, blocking collectives, shards(): everyone = lax.all_gather(points, 'cent', axis=0, tiled=True)  25.7 us
    dot_general x1, matrix products, shards(): lax.dot_general(onehot, moved, (((0,), (0,)), ((), ())), preferred_elemen...  22.7 us
    all_gather x1, blocking collectives, shards(): terms = lax.all_gather(block_2, 'cent')  17.2 us
    dot_general x1, matrix products, accumulate(): lax.dot_general(resp.astype(jnp.bfloat16), block, (((0,), (0,)), ((), ())...  12.1 us
    dot_general x1, matrix products, logits_of(): lax.dot_general(block, centroids, (((1,), (1,)), ((), ())), preferred_ele...  8.45 us
  transfers between devices with their start and end apart: 1, of which 1 were waited for; matrix products, arithmetic and copies ran while one was open for 3% of the time, Pallas kernels for 0%

profile of v1, /device:TPU:0, one launch (start us, length us, event | category | flops | bytes accessed | tf_op | source)
XLA Modules:
  0.0 225.5 jit_solution(10477984378221761078)
XLA Ops:
  7.2 0.0 reduce-scatter.2.cloned.1.call-start
  7.2 25.7 %all_gather.9 = bf16[512,768]{1,0:T(8,128)(2,1)S(1)} all-gather(bf16[32,768]{1,0:T(8,128)(2,1)} %param.4), channel_id=1, replica_groups=mesh['groups'=2,'cent'=16] {'cent'}, dimensions={0}, use_global_device_ids=true | all-gather | bytes 835584 | tf_op jit(solution)/shard_map/all_gather | solution.py:16
  32.9 8.4 %multiply_reduce_fusion = (f32[512]{0:T(512)S(1)}, f32[512,4096]{1,0:T(8,128)}) fusion(bf16[512,768]{1,0:T(8,128)(2,1)S(1)} %all_gather.9, bf16[4096,768]{1,0:T(8,128)(2,1)} %param.5), kind=kOutput, calls=%fused_computation.9 | convolution fusion | flops 3225419264 | bytes 15468544 | tf_op jit(solution)/shard_map/while/body/eval_jaxpr/dot_general | solution.py:24
  41.4 29.8 %pmax.7 = f32[512]{0:T(512)S(1)} all-reduce(f32[512]{0:T(512)S(1)} %get-tuple-element.24), channel_id=1, replica_groups=mesh['groups'=2,'cent'=16] {'cent'}, use_global_device_ids=true, to_apply=%region_1.0 | all-reduce | flops 512 | bytes 4096 | tf_op jit(solution)/shard_map/pmax | solution.py:38
  71.2 4.9 %exponential_reduce_fusion = f32[512]{0:T(512)S(1)} fusion(f32[512,4096]{1,0:T(8,128)} %get-tuple-element.25, f32[512]{0:T(512)S(1)} %get-tuple-element.24), kind=kLoop, calls=%fused_computation.7 | loop fusion | flops 6290944 | bytes 8392704 | tf_op jit(solution)/shard_map/while/body/eval_jaxpr/reduce_sum | solution.py:33
  76.1 17.2 %all-gather.1 = f32[16,1,512]{2,1,0:T(1,128)S(1)} all-gather(f32[1,1,512]{2,1,0:T(1,128)S(1)} %bitcast.8), channel_id=2, replica_groups=mesh['groups'=2,'cent'=16] {'cent'}, dimensions={0}, use_global_device_ids=true | all-gather | bytes 34816 | tf_op jit(solution)/shard_map/all_gather | solution.py:40
  93.3 4.5 %fusion.11 = f32[4096]{0:T(1024)S(1)} fusion(f32[512]{0:T(512)S(1)} %reduce_sum.41, f32[512]{0:T(512)S(1)} %pmax.7, f32[512,4096]{1,0:T(8,128)} %get-tuple-element.25), kind=kLoop, calls=%fused_computation.22 | loop fusion | flops 8384512 | bytes 8409088 | tf_op jit(solution)/shard_map/while/body/eval_jaxpr/reduce_sum | solution.py:48
  97.8 0.0 copy-start.1
  97.8 12.1 %fusion.12 = (bf16[4096,768]{1,0:T(8,128)(2,1)}, f32[4096,768]{1,0:T(8,128)}) fusion(f32[4096]{0:T(1024)S(1)} %broadcast_add_fusion, bf16[4096,768]{1,0:T(8,128)(2,1)} %param.5, bf16[512,768]{1,0:T(8,128)(2,1)S(1)} %all_gather.9, f32[512]{0:T(512)S(1)} %reduce_sum.41, f32[512]{0:T(512)S(1)} %pmax.7, f32[512,4096]{1,0:T(8,128)} %get-tuple-element.25), kind=kOutput, calls=%fused_computation.23 | convolution fusion | flops 3245342720 | bytes 34361344 | tf_op jit(solution)/shard_map/while/body/eval_jaxpr/dot_general | solution.py:49
  109.9 0.0 copy-done.1
  109.9 0.0 copy-start.2
  109.9 22.7 %fusion.1 = f32[2048,768]{1,0:T(8,128)} fusion(s32[4096]{0:T(1024)S(1)} %copy-done.1, f32[4096,768]{1,0:T(8,128)} %get-tuple-element.34, f32[4096]{0:T(1024)S(1)} %fusion.11), kind=kOutput, calls=%fused_computation.2 | convolution fusion | flops 12899581952 | bytes 18907136 | tf_op jit(solution)/shard_map/dot_general | solution.py:65
  132.6 0.0 copy-start
  132.6 0.0 reduce-scatter.2.cloned.1.call-update
  132.7 0.0 copy-done.2
  132.7 0.6 dynamic-slice.3
  134.0 5.9 %fusion.6 = f32[2048]{0:T(1024)S(1)} fusion(s32[4096]{0:T(1024)S(1)} %copy-done.1, bf16[1,4096]{1,0:T(2,128)(2,1)S(1)} %subtract_convert_fusion, bf16[1,4096]{1,0:T(2,128)(2,1)S(1)} %convert_element_type.52), kind=kOutput, calls=%fused_computation.12 | convolution fusion | flops 41977856 | bytes 40960 | tf_op jit(solution)/shard_map/dot_general | solution.py:69
  139.8 32.9 %all-reduce = f32[2048]{0:T(1024)S(1)} all-reduce(f32[2048]{0:T(1024)S(1)} %fusion.6), channel_id=4, replica_groups=mesh['groups'=2,'cent'=16] {'cent'}, use_global_device_ids=true, to_apply=%region_7.8.clone | all-reduce | flops 2048 | bytes 16384
  172.7 0.1 dynamic-slice_add_fusion
  172.8 43.9 %reduce-scatter.2.cloned.1.call-done = f32[128,768]{1,0:T(8,128)} async-done(((f32[2048,768]{1,0:T(8,128)}), f32[128,768]{1,0:T(8,128)}) %reduce-scatter.2.cloned.1.call-update) | async-done | bytes 393232 | tf_op jit(solution)/shard_map/reduce_scatter | solution.py:71
  216.8 0.0 copy-done
  216.8 1.8 add_divide_fusion.1
  (5 shorter events, 0.1 us)
Async XLA Ops:
  7.2 209.6 %reduce-scatter.2.cloned.1.call-start = ((), (), s32[]{:S(2)}) async-start(), calls=%async_computation.1 | async-start | bytes 6684672 | tf_op jit(solution)/shard_map/reduce_scatter | solution.py:71
  97.8 12.1 %copy-start.1 = (s32[4096]{0:T(1024)S(1)}, s32[4096]{0:T(1024)}, u32[]{:S(2)}) copy-start(s32[4096]{0:T(1024)} %param.7) | copy-start | bytes 49156
  109.9 22.8 %copy-start.2 = (u32[32]{0:T(128)S(1)}, u32[32]{0:T(128)}, u32[]{:S(2)}) copy-start(u32[32]{0:T(128)} %constant.43) | copy-start | bytes 388
  132.6 84.1 %copy-start = (f32[128,768]{1,0:T(8,128)S(1)}, f32[128,768]{1,0:T(8,128)}, u32[]{:S(2)}) copy-start(f32[128,768]{1,0:T(8,128)} %param.6) | copy-start | bytes 1179652
Sparse Core Ops, SparseCore 0:
  132.8 83.9 reduce-scatter.1
